TPU v7x, 64 devices: a 2x2x8 block of a 4x4x8 slice. The times are simulated.
64 devices in a mesh: rep: 8 (over x, y, core), dp: 8 (over z).
Axes of the slice: x: 2, y: 2, z: 8, core: 2. Of those that a mesh axis runs over, the one named last changes fastest.
The devices are a block of a 4x4x8 slice.
Arguments:
- x: bfloat16 [64, 4096, 512], P(('rep', 'dp')), parts along dimension 0
- dy: bfloat16 [64, 4096, 512], P(('rep', 'dp')), parts along dimension 0
- w_gate: bfloat16 [2, 512, 1408], P(None, 'dp')
- w_up: bfloat16 [2, 512, 1408], P(None, 'dp')
- w_down: bfloat16 [2, 1408, 512], P(None, 'dp')
- m_w_gate: float32 [2, 512, 1408], P(None, 'dp')
- m_w_up: float32 [2, 512, 1408], P(None, 'dp')
- m_w_down: float32 [2, 1408, 512], P(None, 'dp')
- v_w_gate: float32 [2, 512, 1408], P(None, 'dp')
- v_w_up: float32 [2, 512, 1408], P(None, 'dp')
- v_w_down: float32 [2, 1408, 512], P(None, 'dp')
Outputs:
- output 1: bfloat16 [16, 512, 1408], P('rep', 'dp'), parts along dimension 0
- output 2: bfloat16 [16, 512, 1408], P('rep', 'dp'), parts along dimension 0
- output 3: bfloat16 [16, 1408, 512], P('rep', 'dp'), parts along dimension 0
- output 4: float32 [16, 512, 1408], P('rep', 'dp'), parts along dimension 0
- output 5: float32 [16, 512, 1408], P('rep', 'dp'), parts along dimension 0
- output 6: float32 [16, 1408, 512], P('rep', 'dp'), parts along dimension 0
- output 7: float32 [16, 512, 1408], P('rep', 'dp'), parts along dimension 0
- output 8: float32 [16, 512, 1408], P('rep', 'dp'), parts along dimension 0
- output 9: float32 [16, 1408, 512], P('rep', 'dp'), parts along dimension 0
There are 8 independent parts. A program takes and returns all parts, laid end to end along the dimension named above; an argument that names none is the same for every part.
All inputs are finite; a program needn't handle non-finite values.
Results may differ from a plain program's by a relative error of at most 0.022.
Values are sent between devices in bfloat16 or wider.
A program may use at most 768 MiB of HBM per device.

v0:
```python
import jax
import jax.numpy as jnp
from jax import lax
from jax.sharding import PartitionSpec as P

NAMES = ("w_gate", "w_up", "w_down")


def matmul(a, w):
    return jnp.dot(a, w, preferred_element_type=jnp.float32).astype(jnp.bfloat16)


def normed(h):
    wide = h.astype(jnp.float32)
    scale = lax.rsqrt(jnp.mean(wide**2, -1, keepdims=True) + 1e-6)
    return (wide * scale).astype(jnp.bfloat16)


def layer(h, w):
    a = normed(h)
    gate = jnp.dot(a, w["w_gate"], preferred_element_type=jnp.float32)
    up = jnp.dot(a, w["w_up"], preferred_element_type=jnp.float32)
    return h + matmul((jax.nn.silu(gate) * up).astype(jnp.bfloat16), w["w_down"])


def adamw(w, m, v, g):
    m = 0.9 * m + 0.1 * g
    v = 0.95 * v + 0.05 * g * g
    step = m * lax.rsqrt(v + 1e-8) + 0.1 * w
    return (w - 0.02 * step).astype(jnp.bfloat16), m, v


def clipped(gradients, sum_of_squares, count):
    factor = jnp.minimum(1.0, 0.5 * lax.rsqrt(sum_of_squares / count + 1e-30))
    return [g * factor for g in gradients]


def solution(mesh):
    def fetched(weights, number):
        return {name: lax.all_gather(w[number], "dp", axis=0, tiled=True) for name, w in zip(NAMES, weights, strict=True)}

    def step(x, dy, *arrays):
        weights, m, v = (arrays[i : i + 3] for i in (0, 3, 6))
        layers = weights[0].shape[0]
        h, kept = x[0], []
        for number in range(layers):
            kept.append(h)
            h = layer(h, fetched(weights, number))
        by_h, mine = dy[0], [None] * layers
        for number in reversed(range(layers)):
            _, back = jax.vjp(lambda w, h: layer(h, w), fetched(weights, number), kept[number])
            by_w, by_h = back(by_h)
            mine[number] = [lax.psum_scatter(by_w[name], "dp", scatter_dimension=0, tiled=True) for name in NAMES]
        gradients = [jnp.stack([mine[number][i] for number in range(layers)]).astype(jnp.float32) for i in range(3)]
        squares = lax.psum(sum(jnp.sum(g * g) for g in gradients), "dp")
        gradients = clipped(gradients, squares, lax.psum(1, "dp") * sum(g.size for g in gradients))
        new = [adamw(w.astype(jnp.float32), m, v, g) for w, m, v, g in zip(weights, m, v, gradients, strict=True)]
        return tuple(one[which] for which in range(3) for one in new)

    states, cut = P(("rep", "dp"), None, None), P(None, "dp", None)
    return jax.shard_map(
        step,
        mesh=mesh,
        in_specs=(states, states) + (cut,) * 9,
        out_specs=(P("rep", "dp", None),) * 9,
        check_vma=False,
    )
```

profile of v0, /device:TPU:30, one launch (start us, length us, event | category | flops | bytes accessed | tf_op | source)
XLA Modules:
  0.0 562.6 jit_solution(8896384039293649999)
XLA Ops:
  14.9 6.4 %copy.20 = bf16[1,4096,512]{1,2,0:T(8,128)(2,1)} copy(bf16[1,4096,512]{2,1,0:T(8,128)(2,1)} %param.11) | data formatting | bytes 8388608 | tf_op args[0]
  21.3 3.1 fusion.15
  24.4 6.4 %copy.21 = bf16[1,4096,512]{1,2,0:T(8,128)(2,1)} copy(bf16[1,4096,512]{2,1,0:T(8,128)(2,1)} %param.12) | data formatting | bytes 8388608 | tf_op args[1]
  30.8 18.6 %all-gather.13.cloned.1.call-done = bf16[1,512,1408]{2,1,0:T(8,128)(2,1)} async-done(((bf16[1,64,1408]{2,1,0:T(8,128)(2,1)}), bf16[1,512,1408]{2,1,0:T(8,128)(2,1)}) %all-gather.13.cloned.1.call-update) | async-done | bytes 1441808 | tf_op jit(solution)/shard_map/all_gather | solution.py:40
  49.4 13.2 %fusion.47 = f32[4096,1408]{1,0:T(8,128)} fusion(bf16[1,4096,512]{1,2,0:T(8,128)(2,1)} %copy.20, f32[4096]{0:T(1024)S(1)} %add_rsqrt_fusion, bf16[1,512,1408]{2,1,0:T(8,128)(2,1)} %all-gather.13.cloned.1.call-done), kind=kOutput, calls=%fused_computation.57 | convolution fusion | flops 5911871488 | bytes 28721152 | tf_op jit(solution)/shard_map/dot_general | solution.py:21
  62.6 23.5 %all-gather.15.cloned.1.call-done = bf16[1,512,1408]{2,1,0:T(8,128)(2,1)} async-done(((bf16[1,64,1408]{2,1,0:T(8,128)(2,1)}), bf16[1,512,1408]{2,1,0:T(8,128)(2,1)}) %all-gather.15.cloned.1.call-update) | async-done | bytes 1441808 | tf_op jit(solution)/shard_map/all_gather | solution.py:40
  86.1 24.3 %multiply_convert_fusion.1 = (bf16[4096,1408]{1,0:T(8,128)(2,1)}, f32[4096,1408]{1,0:T(8,128)}) fusion(f32[4096,1408]{1,0:T(8,128)} %fusion.47, bf16[1,512,1408]{2,1,0:T(8,128)(2,1)} %all-gather.15.cloned.1.call-done, bf16[1,4096,512]{1,2,0:T(8,128)(2,1)} %copy.20, f32[4096]{0:T(1024)S(1)} %add_rsqrt_fusion), kind=kOutput, calls=%fused_computation.17 | convolution fusion | flops 5946474496 | bytes 63324160 | tf_op jit(solution)/shard_map/dot_general | solution.py:22
  110.5 12.4 %all-gather.17.cloned.1.call-done = bf16[1,1408,512]{2,1,0:T(8,128)(2,1)} async-done(((bf16[1,176,512]{2,1,0:T(8,128)(2,1)}), bf16[1,1408,512]{2,1,0:T(8,128)(2,1)}) %all-gather.17.cloned.1.call-update) | async-done | bytes 1441808 | tf_op jit(solution)/shard_map/all_gather | solution.py:40
  122.9 12.5 %fusion.19 = (f32[4096]{0:T(1024)S(1)}, bf16[4096,512]{0,1:T(8,128)(2,1)}) fusion(bf16[4096,1408]{1,0:T(8,128)(2,1)} %get-tuple-element.24, bf16[1,1408,512]{2,1,0:T(8,128)(2,1)} %all-gather.17.cloned.1.call-done, bf16[1,4096,512]{1,2,0:T(8,128)(2,1)} %copy.20), kind=kOutput, calls=%fused_computation.37 | convolution fusion | flops 5916061696 | bytes 21381120 | tf_op jit(solution)/shard_map/dot_general | solution.py:10
  136.0 23.4 %all-gather.21.cloned.1.call-done = bf16[1,1408,512]{2,1,0:T(8,128)(2,1)} async-done(((bf16[1,176,512]{2,1,0:T(8,128)(2,1)}), bf16[1,1408,512]{2,1,0:T(8,128)(2,1)}) %all-gather.21.cloned.1.call-update) | async-done | bytes 1441808 | tf_op jit(solution)/shard_map/all_gather | solution.py:40
  159.4 12.0 %convolution_convert_fusion.1 = bf16[4096,1408]{1,0:T(8,128)(2,1)} fusion(bf16[1,4096,512]{2,1,0:T(8,128)(2,1)} %param.12, bf16[1,1408,512]{2,1,0:T(8,128)(2,1)} %all-gather.21.cloned.1.call-done), kind=kOutput, calls=%fused_computation.23 | convolution fusion | flops 5911347200 | bytes 17170432 | tf_op jit(solution)/shard_map/transpose(jvp())/dot_general | solution.py:10
  171.4 24.6 %all-gather.23.cloned.1.call-done = bf16[1,512,1408]{2,1,0:T(8,128)(2,1)} async-done(((bf16[1,64,1408]{2,1,0:T(8,128)(2,1)}), bf16[1,512,1408]{2,1,0:T(8,128)(2,1)}) %all-gather.23.cloned.1.call-update) | async-done | bytes 1441808 | tf_op jit(solution)/shard_map/all_gather | solution.py:40
  196.0 13.1 %fusion.39 = f32[4096,1408]{1,0:T(8,128)} fusion(bf16[4096,512]{0,1:T(8,128)(2,1)} %get-tuple-element.27, f32[4096]{0:T(1024)S(1)} %fusion.79, bf16[1,512,1408]{2,1,0:T(8,128)(2,1)} %all-gather.23.cloned.1.call-done), kind=kOutput, calls=%fused_computation.54 | convolution fusion | flops 5911871488 | bytes 28721152 | tf_op jit(solution)/shard_map/jvp()/dot_general | solution.py:22
  209.1 23.5 %all-gather.19.cloned.1.call-done = bf16[1,512,1408]{2,1,0:T(8,128)(2,1)} async-done(((bf16[1,64,1408]{2,1,0:T(8,128)(2,1)}), bf16[1,512,1408]{2,1,0:T(8,128)(2,1)}) %all-gather.19.cloned.1.call-update) | async-done | bytes 1441808 | tf_op jit(solution)/shard_map/all_gather | solution.py:40
  232.5 31.8 %fusion.2 = (bf16[4096,1408]{1,0:T(8,128)(2,1)}, f32[4096,1408]{1,0:T(8,128)}) fusion(f32[4096,1408]{1,0:T(8,128)} %fusion.39, bf16[4096,1408]{1,0:T(8,128)(2,1)} %convolution_convert_fusion.1, bf16[1,512,1408]{2,1,0:T(8,128)(2,1)} %all-gather.19.cloned.1.call-done, bf16[4096,512]{0,1:T(8,128)(2,1)} %get-tuple-element.27, f32[4096]{0:T(1024)S(1)} %fusion.79), kind=kOutput, calls=%fused_computation.8 | convolution fusion | flops 5981077504 | bytes 74858496 | tf_op jit(solution)/shard_map/jvp()/dot_general | solution.py:21
  264.4 12.8 %convolution_convert_fusion.5 = bf16[512,1408]{1,0:T(8,128)(2,1)} fusion(bf16[4096,1408]{1,0:T(8,128)(2,1)} %get-tuple-element.28, bf16[4096,512]{0,1:T(8,128)(2,1)} %get-tuple-element.27, f32[4096]{0:T(1024)S(1)} %fusion.79), kind=kOutput, calls=%fused_computation.53 | convolution fusion | flops 5911871488 | bytes 17186816 | tf_op jit(solution)/shard_map/transpose(jvp())/dot_general | solution.py:21
  277.3 17.2 %fusion.22 = bf16[4096,512]{0,1:T(8,128)(2,1)} fusion(bf16[4096,1408]{1,0:T(8,128)(2,1)} %convolution_convert_fusion.1, bf16[1,512,1408]{2,1,0:T(8,128)(2,1)} %all-gather.23.cloned.1.call-done, f32[4096,1408]{1,0:T(8,128)} %get-tuple-element.29), kind=kOutput, calls=%fused_computation.40 | convolution fusion | flops 5942280192 | bytes 40239104 | tf_op jit(solution)/shard_map/transpose(jvp())/dot_general | solution.py:22
  294.6 11.1 %fusion.21 = (f32[4096]{0:T(1024)S(1)}, bf16[4096,512]{0,1:T(8,128)(2,1)S(1)}) fusion(bf16[4096,512]{0,1:T(8,128)(2,1)S(1)} %copy-done.1, bf16[4096,512]{0,1:T(8,128)(2,1)} %fusion.22, bf16[4096,1408]{1,0:T(8,128)(2,1)} %get-tuple-element.28, bf16[1,512,1408]{2,1,0:T(8,128)(2,1)} %all-gather.19.cloned.1.call-done), kind=kOutput, calls=%fused_computation.39 | convolution fusion | flops 5916061696 | bytes 25575424 | tf_op jit(solution)/shard_map/transpose(jvp())/dot_general | solution.py:21
  305.8 2.9 fusion.25
  308.7 9.5 %convolution_convert_fusion = bf16[4096,1408]{1,0:T(8,128)(2,1)} fusion(bf16[4096,512]{0,1:T(8,128)(2,1)S(1)} %fusion.25, bf16[1,1408,512]{2,1,0:T(8,128)(2,1)S(1)} %copy-done.13), kind=kOutput, calls=%fused_computation.22 | convolution fusion | flops 5911347200 | bytes 17170432 | tf_op jit(solution)/shard_map/transpose(jvp())/dot_general | solution.py:10
  318.2 24.5 %fusion.33 = bf16[512,1408]{1,0:T(8,128)(2,1)} fusion(f32[4096,1408]{1,0:T(8,128)} %fusion.47, f32[4096,1408]{1,0:T(8,128)} %get-tuple-element.25, bf16[4096,1408]{1,0:T(8,128)(2,1)} %convolution_convert_fusion, bf16[1,4096,512]{1,2,0:T(8,128)(2,1)} %copy.20, f32[4096]{0:T(1024)S(1)} %copy-done.12), kind=kOutput, calls=%fused_computation.50 | convolution fusion | flops 5976031232 | bytes 63324160 | tf_op jit(solution)/shard_map/transpose(jvp())/dot_general | solution.py:21
  342.9 17.3 %fusion.32 = bf16[512,1408]{1,0:T(8,128)(2,1)} fusion(bf16[4096,1408]{1,0:T(8,128)(2,1)} %convolution_convert_fusion.1, bf16[4096,512]{0,1:T(8,128)(2,1)} %get-tuple-element.27, f32[4096]{0:T(1024)S(1)} %fusion.79, f32[4096,1408]{1,0:T(8,128)} %get-tuple-element.29), kind=kOutput, calls=%fused_computation.49 | convolution fusion | flops 5947195392 | bytes 40255488 | tf_op jit(solution)/shard_map/transpose(jvp())/dot_general | solution.py:22
  360.3 17.6 %fusion.36 = bf16[512,1408]{1,0:T(8,128)(2,1)} fusion(bf16[4096,1408]{1,0:T(8,128)(2,1)} %convolution_convert_fusion, f32[4096,1408]{1,0:T(8,128)} %fusion.47, bf16[1,4096,512]{1,2,0:T(8,128)(2,1)} %copy.20, f32[4096]{0:T(1024)S(1)} %copy-done.12), kind=kOutput, calls=%fused_computation.51 | convolution fusion | flops 5947195392 | bytes 40255488 | tf_op jit(solution)/shard_map/transpose(jvp())/dot_general | solution.py:22
  378.0 20.4 %fusion.29 = bf16[1408,512]{1,0:T(8,128)(2,1)} fusion(bf16[1,4096,512]{2,1,0:T(8,128)(2,1)} %param.12, f32[4096,1408]{1,0:T(8,128)} %fusion.39, f32[4096,1408]{1,0:T(8,128)} %get-tuple-element.29), kind=kOutput, calls=%fused_computation.48 | convolution fusion | flops 5940903936 | bytes 51773440 | tf_op jit(solution)/shard_map/transpose(jvp())/dot_general | solution.py:10
  398.7 12.6 %convolution_convert_fusion.4 = bf16[1408,512]{1,0:T(8,128)(2,1)} fusion(bf16[4096,1408]{1,0:T(8,128)(2,1)} %get-tuple-element.24, bf16[4096,512]{0,1:T(8,128)(2,1)} %copy-done.2), kind=kOutput, calls=%fused_computation.52 | convolution fusion | flops 5906300928 | bytes 17170432 | tf_op jit(solution)/shard_map/transpose(jvp())/dot_general | solution.py:10
  413.1 3.3 reduce-scatter.13.cloned.1.call-done
  416.4 37.7 %reduce-scatter.11.cloned.1.call-done = bf16[64,1408]{1,0:T(8,128)(2,1)} async-done(((bf16[512,1408]{1,0:T(8,128)(2,1)}), bf16[64,1408]{1,0:T(8,128)(2,1)}) %reduce-scatter.11.cloned.1.call-update) | async-done | bytes 180240 | tf_op jit(solution)/shard_map/reduce_scatter | solution.py:53
  457.2 34.8 %reduce-scatter.17.cloned.1.call-done = bf16[176,512]{1,0:T(8,128)(2,1)} async-done(((bf16[1408,512]{1,0:T(8,128)(2,1)}), bf16[176,512]{1,0:T(8,128)(2,1)}) %reduce-scatter.17.cloned.1.call-update) | async-done | bytes 180240 | tf_op jit(solution)/shard_map/reduce_scatter | solution.py:53
  492.0 37.8 %reduce-scatter.15.cloned.1.call-done = bf16[176,512]{1,0:T(8,128)(2,1)} async-done(((bf16[1408,512]{1,0:T(8,128)(2,1)}), bf16[176,512]{1,0:T(8,128)(2,1)}) %reduce-scatter.15.cloned.1.call-update) | async-done | bytes 180240 | tf_op jit(solution)/shard_map/reduce_scatter | solution.py:53
  532.2 16.2 %psum.7 = f32[]{:T(128)} all-reduce(f32[]{:T(128)S(6)} %add.99), channel_id=1, replica_groups=mesh['rep'=8,'dp'=8] {'dp'}, use_global_device_ids=true, to_apply=%region_12.13 | all-reduce | flops 1 | bytes 8 | tf_op jit(solution)/shard_map/psum | solution.py:55
  549.1 2.4 fusion.75
  551.6 4.0 fusion.66
  (63 shorter events, 14.4 us)
Async XLA Ops:
  7.2 42.3 %all-gather.13.cloned.1.call-start = ((), (), s32[]{:S(2)}) async-start(), calls=%async_computation.12 | async-start | bytes 1622016 | tf_op jit(solution)/shard_map/all_gather | solution.py:40
  9.1 77.1 %all-gather.15.cloned.1.call-start = ((), (), s32[]{:S(2)}) async-start(), calls=%async_computation.13 | async-start | bytes 1622016 | tf_op jit(solution)/shard_map/all_gather | solution.py:40
  11.0 111.9 %all-gather.17.cloned.1.call-start = ((), (), s32[]{:S(2)}) async-start(), calls=%async_computation.14 | async-start | bytes 1622016 | tf_op jit(solution)/shard_map/all_gather | solution.py:40
  12.9 146.5 %all-gather.21.cloned.1.call-start = ((), (), s32[]{:S(2)}) async-start(), calls=%async_computation.16 | async-start | bytes 1622016 | tf_op jit(solution)/shard_map/all_gather | solution.py:40
  13.5 182.4 %all-gather.23.cloned.1.call-start = ((), (), s32[]{:S(2)}) async-start(), calls=%async_computation.17 | async-start | bytes 1622016 | tf_op jit(solution)/shard_map/all_gather | solution.py:40
  14.2 218.4 %all-gather.19.cloned.1.call-start = ((), (), s32[]{:S(2)}) async-start(), calls=%async_computation.15 | async-start | bytes 1622016 | tf_op jit(solution)/shard_map/all_gather | solution.py:40
  14.8 396.5 %reduce-scatter.9.cloned.1.call-start = ((), (), s32[]{:S(2)}) async-start(), calls=%async_computation.7 | async-start | bytes 1622016 | tf_op jit(solution)/shard_map/reduce_scatter | solution.py:53
  24.4 61.8 %copy-start.11 = (f32[4096]{0:T(1024)}, f32[4096]{0:T(1024)S(1)}, u32[]{:S(2)}) copy-start(f32[4096]{0:T(1024)S(1)} %add_rsqrt_fusion) | copy-start | bytes 49156
  135.4 0.6 copy-start.9
  277.2 134.1 %reduce-scatter.7.cloned.1.call-start = ((), (), s32[]{:S(2)}) async-start(), calls=%async_computation.6 | async-start | bytes 1622016 | tf_op jit(solution)/shard_map/reduce_scatter | solution.py:53
  277.3 17.3 %copy-start.1 = (bf16[4096,512]{0,1:T(8,128)(2,1)S(1)}, bf16[4096,512]{0,1:T(8,128)(2,1)}, u32[]{:S(2)}) copy-start(bf16[4096,512]{0,1:T(8,128)(2,1)} %get-tuple-element.27) | copy-start | bytes 12582916
  294.6 11.2 %copy-start.10 = (f32[4096]{0:T(1024)S(1)}, f32[4096]{0:T(1024)}, u32[]{:S(2)}) copy-start(f32[4096]{0:T(1024)} %copy-done.9) | copy-start | bytes 49156
  294.6 11.2 %copy-start = (bf16[1,4096,512]{1,2,0:T(8,128)(2,1)S(1)}, bf16[1,4096,512]{1,2,0:T(8,128)(2,1)}, u32[]{:S(2)}) copy-start(bf16[1,4096,512]{1,2,0:T(8,128)(2,1)} %copy.21) | copy-start | bytes 12582916
  305.8 2.9 copy-start.13
  308.7 9.5 %copy-start.2 = (bf16[4096,512]{0,1:T(8,128)(2,1)}, bf16[4096,512]{0,1:T(8,128)(2,1)S(1)}, u32[]{:S(2)}) copy-start(bf16[4096,512]{0,1:T(8,128)(2,1)S(1)} %fusion.25) | copy-start | bytes 12582916
  308.7 9.5 %copy-start.12 = (f32[4096]{0:T(1024)S(1)}, f32[4096]{0:T(1024)}, u32[]{:S(2)}) copy-start(f32[4096]{0:T(1024)} %copy-done.11) | copy-start | bytes 49156
  342.8 73.6 %reduce-scatter.13.cloned.1.call-start = ((), (), s32[]{:S(2)}) async-start(), calls=%async_computation.9 | async-start | bytes 1622016 | tf_op jit(solution)/shard_map/reduce_scatter | solution.py:53
  360.2 93.9 %reduce-scatter.11.cloned.1.call-start = ((), (), s32[]{:S(2)}) async-start(), calls=%async_computation.8 | async-start | bytes 1622016 | tf_op jit(solution)/shard_map/reduce_scatter | solution.py:53
  378.0 114.0 %reduce-scatter.17.cloned.1.call-start = ((), (), s32[]{:S(2)}) async-start(), calls=%async_computation.11 | async-start | bytes 1622016 | tf_op jit(solution)/shard_map/reduce_scatter | solution.py:53
  398.5 150.6 %copy-start.5 = (bf16[2,176,512]{2,1,0:T(8,128)(2,1)S(1)}, bf16[2,176,512]{2,1,0:T(8,128)(2,1)}, u32[]{:S(2)}) copy-start(bf16[2,176,512]{2,1,0:T(8,128)(2,1)} %param.15) | copy-start | bytes 1081348
  398.5 150.6 %copy-start.6 = (f32[2,176,512]{2,1,0:T(8,128)S(1)}, f32[2,176,512]{2,1,0:T(8,128)}, u32[]{:S(2)}) copy-start(f32[2,176,512]{2,1,0:T(8,128)} %param.21) | copy-start | bytes 2162692
  398.5 150.6 %copy-start.7 = (f32[2,176,512]{2,1,0:T(8,128)S(1)}, f32[2,176,512]{2,1,0:T(8,128)}, u32[]{:S(2)}) copy-start(f32[2,176,512]{2,1,0:T(8,128)} %param.18) | copy-start | bytes 2162692
  398.5 153.0 %copy-start.3 = (bf16[2,64,1408]{2,1,0:T(8,128)(2,1)S(1)}, bf16[2,64,1408]{2,1,0:T(8,128)(2,1)}, u32[]{:S(2)}) copy-start(bf16[2,64,1408]{2,1,0:T(8,128)(2,1)} %param.13) | copy-start | bytes 1081348
  398.6 153.0 %copy-start.4 = (bf16[2,64,1408]{2,1,0:T(8,128)(2,1)S(1)}, bf16[2,64,1408]{2,1,0:T(8,128)(2,1)}, u32[]{:S(2)}) copy-start(bf16[2,64,1408]{2,1,0:T(8,128)(2,1)} %param.14) | copy-start | bytes 1081348
  398.6 153.0 %copy-start.8 = (f32[2,64,1408]{2,1,0:T(8,128)S(1)}, f32[2,64,1408]{2,1,0:T(8,128)}, u32[]{:S(2)}) copy-start(f32[2,64,1408]{2,1,0:T(8,128)} %param.19) | copy-start | bytes 2162692
  398.6 131.2 %reduce-scatter.15.cloned.1.call-start = ((), (), s32[]{:S(2)}) async-start(), calls=%async_computation.10 | async-start | bytes 1622016 | tf_op jit(solution)/shard_map/reduce_scatter | solution.py:53
Sparse Core Ops, SparseCore 0:
  10.2 39.2 all-gather.12
  51.6 34.4 all-gather.14
  88.3 34.5 all-gather.16
  124.9 34.5 all-gather.20
  161.4 34.5 all-gather.22
  198.0 34.5 all-gather.18
  277.4 35.5 reduce-scatter.8
  342.9 35.5 reduce-scatter.6
  380.9 35.5 reduce-scatter.12
  418.6 35.4 reduce-scatter.10
  456.5 35.4 reduce-scatter.16
  494.2 35.5 reduce-scatter.14
where the time goes:
time: 573 us; the launch traced here: 563 us
  matrix products  250 us (44%)
  waiting for transfers between devices  242 us (42%)
  local copies, waits for them, and re-layouts  18.8 us (3%)
  other arithmetic  17.8 us (3%)
  between operations  17.3 us (3%)
  blocking collectives  16.2 us (3%)
    all_gather x6, waiting for transfers between devices, fetched(): lax.all_gather(w[number], 'dp', axis=0, tiled=True)  126 us
    reduce_scatter x6, waiting for transfers between devices, step(): lax.psum_scatter(by_w[name], 'dp', scatter_dimension=0, tiled=True)  114 us
    dot_general x5, matrix products, layer(): gate = jnp.dot(a, w['w_gate'], preferred_element_type=jnp.float32)  93.5 us
    dot_general x5, matrix products, layer(): up = jnp.dot(a, w['w_up'], preferred_element_type=jnp.float32)  89.6 us
    dot_general x5, matrix products, matmul(): jnp.dot(a, w, preferred_element_type=jnp.float32).astype(jnp.bfloat16)  67 us
    psum x1, blocking collectives, step(): squares = lax.psum(sum((jnp.sum(g * g) for g in gradients)), 'dp')  16.2 us
    unnamed x30, local copies, waits for them, and re-layouts  13.5 us
  transfers between devices with their start and end apart: 12, of which 10 were waited for; matrix products, arithmetic and copies ran while one was open for 41% of the time, Pallas kernels for 0%

commit v1 on v0

v1 whole, which is shorter than its diff:
```python
import functools

import jax
import jax.numpy as jnp
from jax import lax
from jax.experimental import pallas as pl
from jax.experimental.pallas import tpu as pltpu
from jax.sharding import PartitionSpec as P

MESH = pl.DeviceIdType.MESH
F32, BF16 = jnp.float32, jnp.bfloat16
SHARE = 32
TILE = 512


def dot(a, b):
    return jnp.dot(a, b, preferred_element_type=F32)


def kernel(n, steps, x_ref, dy_ref, own, g_ref, sq_ref, h, by, byt, a0, a0t, a1, a1t, acc, w, wgut, wdt, part, ring, dgu, ddt, sq, ag_send, ag_recv,
           swap_send, swap_recv, own_sem, in_sem, rs_send, rs_recv, sq_send, sq_recv):
    me, rep = lax.axis_index("dp"), lax.axis_index("rep")
    core = lax.rem(rep, 2)
    sgn = 1 - 2 * core
    tokens, d = h.shape
    tiles = tokens // TILE
    rows_gu = own.shape[1] - SHARE
    width = SHARE * n
    half_rows = own.shape[1] // 2
    half = pl.ds(pl.multiple_of(core * half_rows, 16), half_rows)
    chunks = 2 * steps
    far = n // 2
    slots = ring.shape[0]

    def at(k):
        return lax.rem(k + 2 * n, n)

    def tile(t):
        return pl.ds(pl.multiple_of(t * TILE, TILE), TILE)

    right, left = at(me + sgn), at(me - sgn)
    partner = {"rep": rep + sgn}

    def fetch(t):
        return (
            pltpu.make_async_copy(x_ref.at[tile(t)], h.at[tile(t)], in_sem.at[0, t]),
            pltpu.make_async_copy(dy_ref.at[tile(t)], by.at[tile(t)], in_sem.at[1, t]),
        )

    for t in range(tiles):
        for c in fetch(t):
            c.start()
    own_copy = pltpu.make_async_copy(own.at[:, half], w.at[:, me, half], own_sem)
    own_copy.start()

    barrier = pltpu.get_barrier_semaphore()
    for k in range(1, n):
        pl.semaphore_signal(barrier, inc=1, device_id={"dp": at(me + k)}, device_id_type=MESH)
    pl.semaphore_signal(barrier, inc=1, device_id=partner, device_id_type=MESH)
    pl.semaphore_wait(barrier, n)

    def ag(u, j, long):
        src = at(me - sgn * j) if long else at(me + sgn * j)
        idx = j if long else far + j
        ref = own.at[u, half] if j == 0 else w.at[u, src, half]
        return pltpu.make_async_remote_copy(
            ref, w.at[u, src, half], ag_send.at[u, idx], ag_recv.at[u, idx], device_id={"dp": right if long else left}, device_id_type=MESH
        )

    def ag_arrived(u, j, long):
        src = at(me - sgn * (j + 1)) if long else at(me + sgn * (j + 1))
        idx = j if long else far + j
        ref = w.at[u, src, half]
        pltpu.make_async_remote_copy(
            ref, ref, ag_send.at[u, idx], ag_recv.at[u, idx], device_id={"dp": left if long else right}, device_id_type=MESH
        ).wait_recv()

    def swap(u):
        ref = w.at[u, :, half]
        return pltpu.make_async_remote_copy(ref, ref, swap_send.at[u], swap_recv.at[u], device_id=partner, device_id_type=MESH)

    def ready(u):
        other = pl.ds(pl.multiple_of((1 - core) * half_rows, 16), half_rows)
        ref = w.at[u, :, other]
        pltpu.make_async_remote_copy(ref, ref, swap_send.at[u], swap_recv.at[u], device_id=partner, device_id_type=MESH).wait_recv()

    def when(cond, f):
        if isinstance(cond, bool):
            if cond:
                f()
        else:
            pl.when(cond)(f)

    def both(a, b):
        return (a and b) if isinstance(a, bool) else jnp.logical_and(a, b)

    def stage(i):
        for j in range(far, -1, -1):
            u = i - j

            def hop(u=u, j=j):
                if j > 0:
                    ag_arrived(u, j - 1, True)
                if 0 < j < far:
                    ag_arrived(u, j - 1, False)
                if j < far:
                    ag(u, j, True).start()
                if j < far - 1:
                    ag(u, j, False).start()
                if j == far:
                    if isinstance(u, int):
                        if u == 0:
                            own_copy.wait()
                    swap(u).start()

            when(both(u >= 0, u < chunks), hop)

    def owner(j, long):
        return at(me + sgn * (far - j)) if long else at(me - sgn * (far - 1 - j))

    def rs(q, j, long):
        r, idx = lax.rem(q, slots), j if long else far + j
        src = part.at[lax.rem(q, 3), owner(j, long)] if j == 0 else ring.at[r, idx - 1]
        return pltpu.make_async_remote_copy(
            src, ring.at[r, idx], rs_send.at[r, idx], rs_recv.at[r, idx], device_id={"dp": right if long else left}, device_id_type=MESH
        )

    def rs_arrived(q, j, long):
        r, idx = lax.rem(q, slots), j if long else far + j
        ref = ring.at[r, idx]
        pltpu.make_async_remote_copy(
            ref, ref, rs_send.at[r, idx], rs_recv.at[r, idx], device_id={"dp": left if long else right}, device_id_type=MESH
        ).wait_recv()

    def rs_hop(q, j):
        r = lax.rem(q, slots)
        ways = [True] + [False] * (j < far - 1)
        for long in ways:
            if j > 0:
                rs_arrived(q, j - 1, long)
                idx = j - 1 if long else far + j - 1
                mine = part[lax.rem(q, 3), owner(j, long)].astype(F32)
                ring[r, idx] = (ring[r, idx].astype(F32) + mine).astype(BF16)
        for long in ways:
            rs(q, j, long).start()

    def rs_last(q):
        rs_arrived(q, far - 1, True)
        rs_arrived(q, far - 2, False)
        r = lax.rem(q, slots)
        total = part[lax.rem(q, 3), me].astype(F32) + ring[r, far - 1].astype(F32) + ring[r, 2 * far - 2].astype(F32)
        total = total.astype(BF16)
        g_ref[lax.rem(q + steps, chunks)] = total
        wide = total.astype(F32)
        wide = wide * wide
        sq[...] += jnp.sum(wide.reshape(-1, 8, wide.shape[-1]), axis=0)

    def rs_sent(q):
        for j in range(far):
            rs(q, j, True).wait_send()
        for j in range(far - 1):
            rs(q, j, False).wait_send()

    def rs_middle(q):
        when(both(q >= 2, q < chunks + 2), lambda: rs_hop(q - 2, 3))
        when(both(q >= 1, q < chunks + 1), lambda: rs_hop(q - 1, 1))

    def rs_end(q):
        when(both(q >= 2, q < chunks + 2), lambda: rs_last(q - 2))
        when(both(q >= 1, q < chunks + 1), lambda: rs_hop(q - 1, 2))
        when(both(q >= 0, q < chunks), lambda: rs_hop(q, 0))

    def scale_of(wide):
        return lax.rsqrt(jnp.mean(wide * wide, -1, keepdims=True) + 1e-6)

    def norm_tile(t, src, a, at_):
        wide = src[tile(t)].astype(F32)
        out = (wide * scale_of(wide)).astype(BF16)
        a[tile(t)] = out
        at_[:, tile(t)] = out.T

    def w_gu(u):
        return w[u, :, :rows_gu, :].reshape(n * rows_gu, 2 * width)

    def w_d(u):
        return w[u, :, rows_gu:, :].reshape(width, d)

    sq[...] = jnp.zeros_like(sq)
    stage(0)

    def start_tile(t):
        for c in fetch(t):
            c.wait()
        norm_tile(t, h, a0, a0t)
        byt[:, tile(t)] = by[tile(t)].T

    for i in range(1, far + 1):
        pl.loop(tiles * (i - 1) // far, tiles * i // far)(start_tile)
        stage(i)

    acc[...] = jnp.zeros_like(acc)

    @pl.loop(0, steps)
    def _(s):
        ready(s)

        def forward_tile(t):
            gu = dot(a0[tile(t)], w_gu(s))
            gate, up = gu[:, :width], gu[:, width:]
            act = gate * (0.5 * jnp.tanh(0.5 * gate) + 0.5) * up
            acc[tile(t)] += dot(act.astype(BF16), w_d(s))

        @pl.loop(0, 2)
        def _(part_):
            pl.loop(part_ * (tiles // 2), (part_ + 1) * (tiles // 2))(forward_tile)
            pl.when(part_ == 0)(lambda: stage(s + far + 1))

    @pl.loop(0, tiles)
    def _(t):
        h[tile(t)] = h[tile(t)] + acc[tile(t)].astype(BF16)
        norm_tile(t, h, a1, a1t)

    def backward(first, a, a_t, whole):
        base = steps if whole else 0
        if whole:
            acc[...] = jnp.zeros_like(acc)

        @pl.loop(0, steps)
        def _(s):
            q, u = first + s, base + s
            if whole:
                ready(u)
                wgut[...] = w_gu(u).T
            wdt[...] = w_d(u).T
            dgu[...] = jnp.zeros_like(dgu)
            ddt[...] = jnp.zeros_like(ddt)

            def backward_tile(t):
                gu = dot(a[tile(t)], w_gu(u))
                dact = dot(by[tile(t)], wdt[...]).astype(BF16).astype(F32)
                gate, up = gu[:, :width], gu[:, width:]
                s_ = 0.5 * jnp.tanh(0.5 * gate) + 0.5
                silu = gate * s_
                act = (silu * up).astype(BF16)
                dup = (dact * silu).astype(BF16)
                dgate = (dact * up * (s_ + silu * (1.0 - s_))).astype(BF16)
                both_ = jnp.concatenate([dgate, dup], axis=1)
                dgu[...] += dot(a_t[:, tile(t)], both_)
                ddt[...] += dot(byt[:, tile(t)], act)
                if whole:
                    acc[tile(t)] += dot(both_, wgut[...])

            @pl.loop(0, 2)
            def _(part_):
                pl.loop(part_ * (tiles // 2), (part_ + 1) * (tiles // 2))(backward_tile)

                @pl.when(part_ == 0)
                def _():
                    if whole:
                        stage(u + far + 1)
                    rs_middle(q)

            when(q >= 3, lambda: rs_sent(q - 3))
            p = lax.rem(q, 3)
            part[p, :, :rows_gu, :] = dgu[...].astype(BF16).reshape(n, rows_gu, 2 * width)
            part[p, :, rows_gu:, :] = ddt[...].T.astype(BF16).reshape(n, SHARE, d)
            rs_end(q)

    backward(0, a1, a1t, True)

    @pl.loop(0, tiles)
    def _(t):
        wide = h[tile(t)].astype(F32)
        scale = scale_of(wide)
        ct = acc[tile(t)].astype(BF16).astype(F32)
        back = scale * ct - wide * (scale * scale * scale) * jnp.mean(ct * wide, -1, keepdims=True)
        new = by[tile(t)] + back.astype(BF16)
        by[tile(t)] = new
        byt[:, tile(t)] = new.T

    backward(steps, a0, a0t, False)

    for q in (chunks, chunks + 1):
        rs_middle(q)
        rs_sent(q - 3)
        rs_end(q)
    rs_sent(chunks - 1)

    sq_ref[me] = jnp.sum(sq[...].reshape(8, -1, 128), axis=1)
    for k in range(1, n):
        pltpu.make_async_remote_copy(
            sq_ref.at[me], sq_ref.at[me], sq_send.at[k], sq_recv.at[k], device_id={"dp": at(me + k)}, device_id_type=MESH
        ).start()
    for k in range(1, n):
        ref = sq_ref.at[at(me - k)]
        c = pltpu.make_async_remote_copy(ref, ref, sq_send.at[k], sq_recv.at[k], device_id={"dp": at(me + k)}, device_id_type=MESH)
        c.wait_recv()
    for k in range(1, n):
        ref = sq_ref.at[me]
        pltpu.make_async_remote_copy(ref, ref, sq_send.at[k], sq_recv.at[k], device_id={"dp": at(me + k)}, device_id_type=MESH).wait_send()

    @pl.loop(0, chunks)
    def _(u):
        for j in range(far):
            ag(u, j, True).wait_send()
        for j in range(far - 1):
            ag(u, j, False).wait_send()
        swap(u).wait_send()


def grouped(n, share):
    steps = -(-share // SHARE)
    f = jnp.arange(n * share, dtype=jnp.int32)
    k, r = f // share, f % share
    to = (r // SHARE) * (n * SHARE) + k * SHARE + r % SHARE
    return (to[:, None] == jnp.arange(n * steps * SHARE, dtype=jnp.int32)[None, :]).astype(BF16), steps


def adamw(w, m, v, g):
    m = 0.9 * m + 0.1 * g
    v = 0.95 * v + 0.05 * g * g
    step = m * lax.rsqrt(v + 1e-8) + 0.1 * w
    return (w - 0.02 * step).astype(BF16), m, v


def clipped(gradients, sum_of_squares, count):
    factor = jnp.minimum(1.0, 0.5 * lax.rsqrt(sum_of_squares / count + 1e-30))
    return [g * factor for g in gradients]


def solution(mesh):
    n = mesh.shape["dp"]

    def step(x, dy, *arrays):
        weights, m, v = (arrays[i : i + 3] for i in (0, 3, 6))
        w_gate, w_up, w_down = weights
        layers, rows, _ = w_gate.shape
        share, d = w_down.shape[1:]
        tokens = x.shape[1]
        onehot, steps = grouped(n, share)
        width = n * SHARE
        chunks = layers * steps

        def spread(w):
            w = dot(w.reshape(layers * rows, -1), onehot).astype(BF16)
            return w.reshape(layers, rows, steps, width).transpose(0, 2, 1, 3)

        down = jnp.pad(w_down, ((0, 0), (0, steps * SHARE - share), (0, 0))).reshape(layers, steps, SHARE, d)
        own = jnp.concatenate([jnp.concatenate([spread(w_gate), spread(w_up)], -1), down], 2).reshape(chunks, rows + SHARE, d)

        slots, hops = 4, n - 1
        dma = pltpu.SemaphoreType.DMA
        g, squares = pl.pallas_call(
            functools.partial(kernel, n, steps),
            out_shape=(jax.ShapeDtypeStruct((chunks, rows + SHARE, d), BF16), jax.ShapeDtypeStruct((n, 8, 128), F32)),
            in_specs=[pl.BlockSpec(memory_space=pl.ANY)] * 2 + [pl.BlockSpec(memory_space=pltpu.VMEM)],
            out_specs=(pl.BlockSpec(memory_space=pltpu.VMEM),) * 2,
            scratch_shapes=[
                pltpu.VMEM((tokens, d), BF16),
                pltpu.VMEM((tokens, d), BF16),
                pltpu.VMEM((d, tokens), BF16),
                pltpu.VMEM((tokens, d), BF16),
                pltpu.VMEM((d, tokens), BF16),
                pltpu.VMEM((tokens, d), BF16),
                pltpu.VMEM((d, tokens), BF16),
                pltpu.VMEM((tokens, d), F32),
                pltpu.VMEM((chunks, n, rows + SHARE, d), BF16),
                pltpu.VMEM((2 * width, d), BF16),
                pltpu.VMEM((d, width), BF16),
                pltpu.VMEM((3, n, rows + SHARE, d), BF16),
                pltpu.VMEM((slots, hops, rows + SHARE, d), BF16),
                pltpu.VMEM((d, 2 * width), F32),
                pltpu.VMEM((d, width), F32),
                pltpu.VMEM((8, d), F32),
                dma((chunks, hops)),
                dma((chunks, hops)),
                dma((chunks,)),
                dma((chunks,)),
                dma,
                dma((2, tokens // TILE)),
                dma((slots, hops)),
                dma((slots, hops)),
                dma((n,)),
                dma((n,)),
            ],
            compiler_params=pltpu.CompilerParams(collective_id=0, has_side_effects=True, vmem_limit_bytes=67043328),
            name="step",
        )(x[0], dy[0], own)

        g = g.reshape(layers, steps, rows + SHARE, d)

        def gathered(part):
            part = part.transpose(0, 2, 1, 3).reshape(layers * rows, steps * width)
            return lax.dot_general(part, onehot, (((1,), (1,)), ((), ())), preferred_element_type=F32).reshape(layers, rows, -1)

        gradients = [
            gathered(g[:, :, :rows, :width]),
            gathered(g[:, :, :rows, width:]),
            g[:, :, rows:].reshape(layers, steps * SHARE, d)[:, :share].astype(F32),
        ]
        gradients = clipped(gradients, jnp.sum(squares), n * sum(one.size for one in gradients))
        new = [adamw(w.astype(F32), m, v, g) for w, m, v, g in zip(weights, m, v, gradients, strict=True)]
        return tuple(one[which] for which in range(3) for one in new)

    states, cut = P(("rep", "dp"), None, None), P(None, "dp", None)
    return jax.shard_map(
        step,
        mesh=mesh,
        in_specs=(states, states) + (cut,) * 9,
        out_specs=(P("rep", "dp", None),) * 9,
        check_vma=False,
    )
```

time: 573 us -> 275 us (0.48); the launches traced: 563 us -> 275 us
  Pallas kernels: 0 us -> 251 us
  waiting for transfers between devices: 242 us -> 0 us
  matrix products: 250 us -> 12.5 us
  blocking collectives: 16.2 us -> 0 us
  between operations: 17.3 us -> 1.59 us
  other arithmetic: 17.8 us -> 4.14 us
  local copies, waits for them, and re-layouts: 18.8 us -> 5.33 us
    pallas_call x0 -> x1, Pallas kernels: none -> 251 us  [step(): pl.pallas_call(functools.partial(kernel, n, steps), out_shape=(jax.ShapeD...]
    dot_general x15 -> x4, matrix products: 250 us -> 12.5 us  [the longest x2 8.21 us: gathered(): lax.dot_general(part, onehot, (((1,), (1,)), ((), ())), preferred_element...]
    all_gather x6 -> x0, waiting for transfers between devices: 126 us -> none  [fetched(): lax.all_gather(w[number], 'dp', axis=0, tiled=True)]
    reduce_scatter x6 -> x0, waiting for transfers between devices: 114 us -> none  [step(): lax.psum_scatter(by_w[name], 'dp', scatter_dimension=0, tiled=True)]
    psum x1 -> x0, blocking collectives: 16.2 us -> none  [step(): squares = lax.psum(sum((jnp.sum(g * g) for g in gradients)), 'dp')]
    unnamed x30 -> x24, local copies, waits for them, and re-layouts: 13.5 us -> 0.18 us
    reduce_sum x4 -> x1, other arithmetic: 8.46 us -> 1.37 us  [step(): jnp.sum(squares)]
  transfers between devices with their start and end apart: 12 -> 0, of which waited for: 10 -> 0; matrix products, arithmetic and copies ran while one was open for 41% -> 0% of each run, Pallas kernels for 0% -> 0%
where the time goes in v1:
time: 275 us
  Pallas kernels  251 us (91%)
  matrix products  12.5 us (5%)
  local copies, waits for them, and re-layouts  5.33 us (2%)
  other arithmetic  4.14 us (2%)
    pallas_call x1, Pallas kernels, step(): pl.pallas_call(functools.partial(kernel, n, steps), out_shape=(jax.ShapeD...  251 us
    dot_general x2, matrix products, gathered(): lax.dot_general(part, onehot, (((1,), (1,)), ((), ())), preferred_element...  8.21 us

profile of v1, /device:TPU:30, one launch (start us, length us, event | category | flops | bytes accessed | tf_op | source)
XLA Modules:
  0.0 275.0 jit_solution(11420846755857410522)
XLA Ops:
  0.7 0.0 copy-start.4
  0.7 0.0 copy-start.10
  0.7 2.7 fusion.26
  3.4 0.2 copy.25
  3.6 0.4 reshape.99
  4.0 1.7 fusion.29
  5.7 0.2 copy.24
  5.9 0.0 copy-start
  5.9 0.4 reshape.97
  6.3 0.2 pad_maximum_fusion.1
  6.5 0.2 copy.26
  6.8 0.1 copy-done
  6.9 1.1 pad_maximum_fusion.own
  8.0 251.4 %step.1 = (bf16[12,96,512]{2,1,0:T(8,128)(2,1)}, f32[8,8,128]{2,1,0:T(8,128)}) custom-call(bf16[4096,512]{1,0:T(8,128)(2,1)} %bitcast.34, bf16[4096,512]{1,0:T(8,128)(2,1)} %bitcast.35, bf16[12,96,512]{2,1,0:T(8,128)(2,1)} %pad_maximum_fusion.own), custom_call_target="tpu_custom_call" | custom-call | tf_op jit(solution)/shard_map/step/pallas_call | solution.py:353
  259.4 1.4 reduce_sum.9
  261.4 1.0 slice.18
  262.5 0.0 copy-start.5
  262.5 0.0 copy-start.6
  262.5 0.0 copy-start.7
  262.5 1.3 fusion.65
  263.8 0.5 copy_bitcast_fusion
  264.3 0.4 dot_general.20
  264.7 0.4 dot_general.18
  265.2 0.0 copy-start.8
  265.2 0.0 copy-start.9
  265.2 0.0 copy-start.11
  265.2 4.7 %fusion.34 = (bf16[2,64,1408]{2,1,0:T(8,128)(2,1)}, f32[2,64,1408]{2,1,0:T(8,128)}, f32[2,64,1408]{2,1,0:T(8,128)}) fusion(bf16[2,64,1408]{2,1,0:T(8,128)(2,1)} %param.13, f32[2,64,1408]{2,1,0:T(8,128)S(1)} %copy-done.6, f32[2,64,1408]{2,1,0:T(8,128)S(1)} %copy-done.7, f32[]{:T(128)S(6)} %min_shard_map.3, bf16[2,64,1536]{2,1,0:T(8,128)(2,1)S(1)} %dot_general.18, ...), kind=kOutput, calls=%fused_computation.30 | convolution fusion | flops 558694400 | bytes 4003332 | tf_op jit(solution)/shard_map/dot_general | solution.py:394
  269.9 0.0 copy-start.1
  269.9 0.0 copy-start.2
  269.9 0.0 copy-start.3
  270.0 3.5 %fusion.37 = (bf16[2,64,1408]{2,1,0:T(8,128)(2,1)}, f32[2,64,1408]{2,1,0:T(8,128)}, f32[2,64,1408]{2,1,0:T(8,128)}) fusion(bf16[2,64,1408]{2,1,0:T(8,128)(2,1)S(1)} %copy-done.11, f32[2,64,1408]{2,1,0:T(8,128)S(1)} %copy-done.8, f32[2,64,1408]{2,1,0:T(8,128)S(1)} %copy-done.9, f32[]{:T(128)S(6)} %min_shard_map.3, bf16[2,64,1536]{2,1,0:T(8,128)(2,1)S(1)} %dot_general.20, ...), kind=kOutput, calls=%fused_computation.33 | convolution fusion | flops 558694400 | bytes 4003332 | tf_op jit(solution)/shard_map/dot_general | solution.py:394
  273.5 1.4 fusion.40
  (13 shorter events, 0.1 us)
Async XLA Ops:
  0.7 3.3 %copy-start.4 = (s32[1408]{0:T(1024)}, s32[1408]{0:T(1024)S(1)}, u32[]{:S(2)}) copy-start(s32[1408]{0:T(1024)S(1)} %fusion.52) | copy-start | bytes 16900
  0.7 3.3 %copy-start.10 = (bf16[2,64,1408]{2,1,0:T(8,128)(2,1)S(1)}, bf16[2,64,1408]{2,1,0:T(8,128)(2,1)}, u32[]{:S(2)}) copy-start(bf16[2,64,1408]{2,1,0:T(8,128)(2,1)} %param.13) | copy-start | bytes 1081348
  5.9 1.0 copy-start
  262.5 2.7 copy-start.5
  262.5 2.7 copy-start.6
  262.5 2.7 copy-start.7
  265.2 4.7 %copy-start.8 = (f32[2,64,1408]{2,1,0:T(8,128)S(1)}, f32[2,64,1408]{2,1,0:T(8,128)}, u32[]{:S(2)}) copy-start(f32[2,64,1408]{2,1,0:T(8,128)} %param.20) | copy-start | bytes 2162692
  265.2 4.7 %copy-start.9 = (f32[2,64,1408]{2,1,0:T(8,128)S(1)}, f32[2,64,1408]{2,1,0:T(8,128)}, u32[]{:S(2)}) copy-start(f32[2,64,1408]{2,1,0:T(8,128)} %param.17) | copy-start | bytes 2162692
  265.2 4.7 %copy-start.11 = (bf16[2,64,1408]{2,1,0:T(8,128)(2,1)S(1)}, bf16[2,64,1408]{2,1,0:T(8,128)(2,1)}, u32[]{:S(2)}) copy-start(bf16[2,64,1408]{2,1,0:T(8,128)(2,1)} %param.14) | copy-start | bytes 1081348
  269.9 3.6 %copy-start.1 = (bf16[2,176,512]{2,1,0:T(8,128)(2,1)S(1)}, bf16[2,176,512]{2,1,0:T(8,128)(2,1)}, u32[]{:S(2)}) copy-start(bf16[2,176,512]{2,1,0:T(8,128)(2,1)} %param.15) | copy-start | bytes 1081348
  269.9 3.6 %copy-start.2 = (f32[2,176,512]{2,1,0:T(8,128)S(1)}, f32[2,176,512]{2,1,0:T(8,128)}, u32[]{:S(2)}) copy-start(f32[2,176,512]{2,1,0:T(8,128)} %param.21) | copy-start | bytes 2162692
  269.9 3.6 %copy-start.3 = (f32[2,176,512]{2,1,0:T(8,128)S(1)}, f32[2,176,512]{2,1,0:T(8,128)}, u32[]{:S(2)}) copy-start(f32[2,176,512]{2,1,0:T(8,128)} %param.18) | copy-start | bytes 2162692

commit v2 on v1

v2 whole, which is shorter than its diff:
```python
import functools

import jax
import jax.numpy as jnp
from jax import lax
from jax.experimental import pallas as pl
from jax.experimental.pallas import tpu as pltpu
from jax.sharding import PartitionSpec as P

MESH = pl.DeviceIdType.MESH
F32, BF16 = jnp.float32, jnp.bfloat16
SHARE = 32
TILE = 512
BIG = 2048


def dot(a, b):
    return jnp.dot(a, b, preferred_element_type=F32)


def dot_nt(a, b):
    return lax.dot_general(a, b, (((1,), (1,)), ((), ())), preferred_element_type=F32)


def kernel(n, steps, x_ref, dy_ref, wg_ref, wu_ref, wd_ref, gg_ref, gu_ref, gd_ref, f_ref, h, by, byt, a0, a0t, a1, a1t, acc, own, w, part, ring, dgu,
           ddt, sq, sq_all, ag_send, ag_recv, swap_send, swap_recv, own_sem, in_sem, rs_send, rs_recv, sq_send, sq_recv):
    me, rep = lax.axis_index("dp"), lax.axis_index("rep")
    core = lax.rem(rep, 2)
    sgn = 1 - 2 * core
    tokens, d = h.shape
    tiles = tokens // TILE
    rows_gu = own.shape[1] - SHARE
    width = SHARE * n
    half_rows = own.shape[1] // 2
    half = pl.ds(pl.multiple_of(core * half_rows, 16), half_rows)
    chunks = 2 * steps
    far = n // 2
    slots = ring.shape[0]

    def at(k):
        return lax.rem(k + 2 * n, n)

    def tile(t):
        return pl.ds(pl.multiple_of(t * TILE, TILE), TILE)

    def cut_by(size):
        return tokens // size, lambda t: pl.ds(pl.multiple_of(t * size, size), size)

    right, left = at(me + sgn), at(me - sgn)
    partner = {"rep": rep + sgn}

    def fetch(t):
        return (
            pltpu.make_async_copy(x_ref.at[tile(t)], h.at[tile(t)], in_sem.at[0, t]),
            pltpu.make_async_copy(dy_ref.at[tile(t)], by.at[tile(t)], in_sem.at[1, t]),
        )

    for t in range(tiles):
        for c in fetch(t):
            c.start()

    barrier = pltpu.get_barrier_semaphore()
    for k in range(1, n):
        pl.semaphore_signal(barrier, inc=1, device_id={"dp": at(me + k)}, device_id_type=MESH)
    pl.semaphore_signal(barrier, inc=1, device_id=partner, device_id_type=MESH)

    layers, rows, hidden = wg_ref.shape
    share = wd_ref.shape[1]
    both_w = jnp.concatenate([wg_ref[...].reshape(layers * rows, hidden), wu_ref[...].reshape(layers * rows, hidden)], 0)
    place = lax.broadcasted_iota(jnp.int32, (1, width), 1)
    unit = lax.broadcasted_iota(jnp.int32, (hidden, width), 0)
    for s in range(steps):
        size = min(SHARE, share - s * SHARE)
        wanted = jnp.where(place < size * n, place // size * share + s * SHARE + place % size, -1)
        pick = jnp.where(unit == wanted, 1.0, 0.0).astype(BF16)
        cut = dot(both_w, pick).astype(BF16).reshape(2, layers, rows, width)
        for l in range(layers):
            block, down = own.at[l * steps + s], wd_ref[l, s * SHARE : s * SHARE + size]
            if size == SHARE:
                block[:rows, :width] = cut[0, l]
                block[:rows, width:] = cut[1, l]
                block[rows:] = down
            else:
                block[:rows, : width // 2] = cut[0, l, :, : width // 2]
                block[:rows, width // 2 : width] = cut[1, l, :, : width // 2]
                block[rows : rows + size, :width] = down[:, :width]
                block[rows + size :, :width] = down[:, width:]
                block[:, width:] = jnp.zeros((rows + SHARE, width), BF16)
    pl.semaphore_wait(barrier, n)
    own_copy = pltpu.make_async_copy(own.at[:, half], w.at[:, me, half], own_sem)
    own_copy.start()

    def sized(c, f):
        if isinstance(c, int):
            f(c % steps == steps - 1)
        else:
            pl.when(lax.rem(c, steps) != steps - 1)(lambda: f(False))
            pl.when(lax.rem(c, steps) == steps - 1)(lambda: f(True))

    def lanes(narrow):
        return pl.ds(0, width if narrow else d)

    def ag(u, j, long, narrow):
        src = at(me - sgn * j) if long else at(me + sgn * j)
        idx = j if long else far + j
        ref = own.at[u, half, lanes(narrow)] if j == 0 else w.at[u, src, half, lanes(narrow)]
        to = w.at[u, src, half, lanes(narrow)]
        return pltpu.make_async_remote_copy(
            ref, to, ag_send.at[u, idx], ag_recv.at[u, idx], device_id={"dp": right if long else left}, device_id_type=MESH
        )

    def ag_arrived(u, j, long, narrow):
        src = at(me - sgn * (j + 1)) if long else at(me + sgn * (j + 1))
        idx = j if long else far + j
        ref = w.at[u, src, half, lanes(narrow)]
        pltpu.make_async_remote_copy(
            ref, ref, ag_send.at[u, idx], ag_recv.at[u, idx], device_id={"dp": left if long else right}, device_id_type=MESH
        ).wait_recv()

    def swap(u, narrow):
        ref = w.at[u, :, half, lanes(narrow)]
        return pltpu.make_async_remote_copy(ref, ref, swap_send.at[u], swap_recv.at[u], device_id=partner, device_id_type=MESH)

    def ready(u, narrow):
        other = pl.ds(pl.multiple_of((1 - core) * half_rows, 16), half_rows)
        ref = w.at[u, :, other, lanes(narrow)]
        pltpu.make_async_remote_copy(ref, ref, swap_send.at[u], swap_recv.at[u], device_id=partner, device_id_type=MESH).wait_recv()

    def when(cond, f):
        if isinstance(cond, bool):
            if cond:
                f()
        else:
            pl.when(cond)(f)

    def both(a, b):
        return (a and b) if isinstance(a, bool) else jnp.logical_and(a, b)

    def stage(i, odd):
        for j in range(far, -1, -1):
            if j % 2 != odd:
                continue
            u = i + (odd - 3 * j) // 2

            def hop(narrow, u=u, j=j):
                if j > 0:
                    ag_arrived(u, j - 1, True, narrow)
                if 0 < j < far:
                    ag_arrived(u, j - 1, False, narrow)
                if j < far:
                    ag(u, j, True, narrow).start()
                if j < far - 1:
                    ag(u, j, False, narrow).start()
                if j == far:
                    if isinstance(u, int):
                        if u == 0:
                            own_copy.wait()
                    swap(u, narrow).start()

            when(both(u >= 0, u < chunks), lambda u=u, hop=hop: sized(u, hop))

    def owner(j, long):
        return at(me + sgn * (far - j)) if long else at(me - sgn * (far - 1 - j))

    def rs(q, j, long, narrow):
        r, idx = lax.rem(q, slots), j if long else far + j
        src = part.at[lax.rem(q, 3), owner(j, long)] if j == 0 else ring.at[r, idx - 1]
        return pltpu.make_async_remote_copy(
            src.at[:, lanes(narrow)],
            ring.at[r, idx, :, lanes(narrow)],
            rs_send.at[r, idx],
            rs_recv.at[r, idx],
            device_id={"dp": right if long else left},
            device_id_type=MESH,
        )

    def rs_arrived(q, j, long, narrow):
        r, idx = lax.rem(q, slots), j if long else far + j
        ref = ring.at[r, idx, :, lanes(narrow)]
        pltpu.make_async_remote_copy(
            ref, ref, rs_send.at[r, idx], rs_recv.at[r, idx], device_id={"dp": left if long else right}, device_id_type=MESH
        ).wait_recv()

    def rs_hop(q, j, narrow):
        r = lax.rem(q, slots)
        ways = [True] + [False] * (j < far - 1)
        for long in ways:
            if j > 0:
                rs_arrived(q, j - 1, long, narrow)
                idx = j - 1 if long else far + j - 1
                mine = part[lax.rem(q, 3), owner(j, long), :, lanes(narrow)].astype(F32)
                ring[r, idx, :, lanes(narrow)] = (ring[r, idx, :, lanes(narrow)].astype(F32) + mine).astype(BF16)
        for long in ways:
            rs(q, j, long, narrow).start()

    def rs_last(q, narrow):
        rs_arrived(q, far - 1, True, narrow)
        rs_arrived(q, far - 2, False, narrow)
        r, cols = lax.rem(q, slots), lanes(narrow)
        total = part[lax.rem(q, 3), me, :, cols].astype(F32) + ring[r, far - 1, :, cols].astype(F32) + ring[r, 2 * far - 2, :, cols].astype(F32)
        total = total.astype(BF16)
        u = lax.rem(q + steps, chunks)
        l = lax.div(u, steps)
        if narrow:
            at_, end = (steps - 1) * width, (steps - 1) * SHARE
            gg_ref[l, :, at_:] = total[:rows_gu, : width // 2]
            gu_ref[l, :, at_:] = total[:rows_gu, width // 2 :]
            gd_ref[l, end:, :width] = total[rows_gu : rows_gu + SHARE // 2]
            gd_ref[l, end:, width:] = total[rows_gu + SHARE // 2 :]
        else:
            s = lax.rem(u, steps)
            gg_ref[l, :, pl.ds(pl.multiple_of(s * width, width), width)] = total[:rows_gu, :width]
            gu_ref[l, :, pl.ds(pl.multiple_of(s * width, width), width)] = total[:rows_gu, width:]
            gd_ref[l, pl.ds(pl.multiple_of(s * SHARE, SHARE), SHARE)] = total[rows_gu:]
        wide = total.astype(F32)
        wide = wide * wide
        sq[:, cols] += jnp.sum(wide.reshape(-1, 8, wide.shape[-1]), axis=0)
        for j in range(far):
            rs(q, j, True, narrow).wait_send()
        for j in range(far - 1):
            rs(q, j, False, narrow).wait_send()

    def rs_slot(q, slot):
        j = 4 - slot
        c = q - j
        when(both(c >= 0, c < chunks), lambda: sized(c, lambda narrow: rs_hop(c, j, narrow)))

    def rs_end(q):
        c = q - 3
        when(both(c >= 0, c < chunks), lambda: sized(c, lambda narrow: rs_last(c, narrow)))

    def scale_of(wide):
        return lax.rsqrt(jnp.mean(wide * wide, -1, keepdims=True) + 1e-6)

    def norm_tile(t, src, a, at_):
        wide = src[tile(t)].astype(F32)
        out = (wide * scale_of(wide)).astype(BF16)
        a[tile(t)] = out
        at_[:, tile(t)] = out.T

    def w_gu(u, narrow):
        return w[u, :, :rows_gu, lanes(narrow)].reshape(n * rows_gu, -1)

    def w_d(u, narrow):
        if not narrow:
            return w[u, :, rows_gu:, :].reshape(width, d)
        mid = rows_gu + SHARE // 2
        return jnp.concatenate([w[u, :, rows_gu:mid, :width].reshape(-1, width), w[u, :, mid:, :width].reshape(-1, width)], 1)

    sq[...] = jnp.zeros_like(sq)
    ahead = 3 * far // 2

    def start_tile(t):
        for c in fetch(t):
            c.wait()
        norm_tile(t, h, a0, a0t)
        byt[:, tile(t)] = by[tile(t)].T

    for i in range(ahead + 1):
        stage(i, 0)
        if 1 <= i <= far:
            pl.loop(tiles * (i - 1) // far, tiles * i // far)(start_tile)
        stage(i, 1)

    acc[...] = jnp.zeros_like(acc)

    def forward(s, narrow):
        ready(s, narrow)
        size = BIG // 2 if narrow else BIG
        count, big = cut_by(size)

        @pl.loop(0, count)
        def _(t):
            gu = dot(a0[big(t)], w_gu(s, narrow))
            units = gu.shape[1] // 2
            gate, up = gu[:, :units], gu[:, units:]
            act = gate * (0.5 * jnp.tanh(0.5 * gate) + 0.5) * up
            acc[big(t)] += dot(act.astype(BF16), w_d(s, narrow))
            pl.when(t == count // 2 - 1)(lambda: stage(s + ahead + 1, 0))
            pl.when(t == count - 1)(lambda: stage(s + ahead + 1, 1))

    @pl.loop(0, steps - 1)
    def _(s):
        forward(s, False)

    forward(steps - 1, True)

    @pl.loop(0, tiles)
    def _(t):
        h[tile(t)] = h[tile(t)] + acc[tile(t)].astype(BF16)
        norm_tile(t, h, a1, a1t)

    def backward(first, a, a_t, whole):
        base = steps if whole else 0
        if whole:
            acc[...] = jnp.zeros_like(acc)

        dgu[...] = jnp.zeros_like(dgu)
        ddt[...] = jnp.zeros_like(ddt)

        def chunk(s, narrow):
            q, u = first + s, base + s
            if whole:
                ready(u, narrow)
            count, big = cut_by(BIG // 2 if narrow else BIG)
            units = width // 2 if narrow else width

            @pl.loop(0, count)
            def _(t):
                gu = dot(a[big(t)], w_gu(u, narrow))
                dact = dot_nt(by[big(t)], w_d(u, narrow)).astype(BF16).astype(F32)
                gate, up = gu[:, :units], gu[:, units:]
                s_ = 0.5 * jnp.tanh(0.5 * gate) + 0.5
                silu = gate * s_
                act = (silu * up).astype(BF16)
                dup = (dact * silu).astype(BF16)
                dgate = (dact * up * (s_ + silu * (1.0 - s_))).astype(BF16)
                both_ = jnp.concatenate([dgate, dup], axis=1)
                dgu[:, : 2 * units] += dot(a_t[:, big(t)], both_)
                ddt[:, :units] += dot(byt[:, big(t)], act)
                if whole:
                    acc[big(t)] += dot_nt(both_, w_gu(u, narrow))
                for slot in (1, 2, 3):

                    @pl.when(t == -(-slot * count // 4) - 1)
                    def _():
                        if whole and slot != 2:
                            for odd in (0, 1):
                                stage(base + ahead + 1 + 2 * s + slot // 2, odd)
                        rs_slot(q, slot)

            rs_end(q)
            p = lax.rem(q, 3)
            part[p, :, :rows_gu, lanes(narrow)] = dgu[:, : 2 * units].astype(BF16).reshape(n, rows_gu, 2 * units)
            down = ddt[:, :units].T.astype(BF16)
            if narrow:
                mid = rows_gu + SHARE // 2
                part[p, :, rows_gu:mid, :width] = down[:, :width].reshape(n, SHARE // 2, width)
                part[p, :, mid:, :width] = down[:, width:].reshape(n, SHARE // 2, width)
            else:
                part[p, :, rows_gu:, :] = down.reshape(n, SHARE, d)
                dgu[...] = jnp.zeros_like(dgu)
                ddt[...] = jnp.zeros_like(ddt)
            rs_hop(q, 0, narrow)

        @pl.loop(0, steps - 1)
        def _(s):
            chunk(s, False)

        chunk(steps - 1, True)

    backward(0, a1, a1t, True)

    @pl.loop(0, tiles)
    def _(t):
        wide = h[tile(t)].astype(F32)
        scale = scale_of(wide)
        ct = acc[tile(t)].astype(BF16).astype(F32)
        back = scale * ct - wide * (scale * scale * scale) * jnp.mean(ct * wide, -1, keepdims=True)
        new = by[tile(t)] + back.astype(BF16)
        by[tile(t)] = new
        byt[:, tile(t)] = new.T

    backward(steps, a0, a0t, False)

    for q in range(chunks, chunks + 3):
        for slot in (1, 2, 3):
            rs_slot(q, slot)
        rs_end(q)

    sq_all[me] = jnp.sum(sq[...].reshape(8, -1, 128), axis=1)
    for k in range(1, n):
        pltpu.make_async_remote_copy(
            sq_all.at[me], sq_all.at[me], sq_send.at[k], sq_recv.at[k], device_id={"dp": at(me + k)}, device_id_type=MESH
        ).start()
    for k in range(1, n):
        ref = sq_all.at[at(me - k)]
        c = pltpu.make_async_remote_copy(ref, ref, sq_send.at[k], sq_recv.at[k], device_id={"dp": at(me + k)}, device_id_type=MESH)
        c.wait_recv()
    for k in range(1, n):
        ref = sq_all.at[me]
        pltpu.make_async_remote_copy(ref, ref, sq_send.at[k], sq_recv.at[k], device_id={"dp": at(me + k)}, device_id_type=MESH).wait_send()

    factor = jnp.minimum(1.0, 0.5 * lax.rsqrt(jnp.sum(sq_all[...]) / (n * layers * (2 * rows * hidden + share * d)) + 1e-30))
    f_ref[...] = jnp.full(f_ref.shape, factor)

    def sent(narrow, u):
        for j in range(far):
            ag(u, j, True, narrow).wait_send()
        for j in range(far - 1):
            ag(u, j, False, narrow).wait_send()
        swap(u, narrow).wait_send()

    @pl.loop(0, chunks)
    def _(u):
        sized(u, lambda narrow: sent(narrow, u))


def grouped(n, share):
    steps = -(-share // SHARE)
    f = jnp.arange(n * share, dtype=jnp.int32)
    k, s, r = f // share, f % share // SHARE, f % share % SHARE
    to = s * (n * SHARE) + k * jnp.minimum(SHARE, share - s * SHARE) + r
    return (to[:, None] == f[None, :]).astype(BF16), steps


def adamw(w, m, v, g):
    m = 0.9 * m + 0.1 * g
    v = 0.95 * v + 0.05 * g * g
    step = m * lax.rsqrt(v + 1e-8) + 0.1 * w
    return (w - 0.02 * step).astype(BF16), m, v


def solution(mesh):
    n = mesh.shape["dp"]

    def step(x, dy, *arrays):
        weights, m, v = (arrays[i : i + 3] for i in (0, 3, 6))
        w_gate, w_up, w_down = weights
        layers, rows, _ = w_gate.shape
        share, d = w_down.shape[1:]
        tokens = x.shape[1]
        onehot, steps = grouped(n, share)
        width = n * SHARE
        chunks = layers * steps

        slots, hops = 5, n - 1
        dma = pltpu.SemaphoreType.DMA
        g_gate, g_up, g_down, factor = pl.pallas_call(
            functools.partial(kernel, n, steps),
            out_shape=(
                jax.ShapeDtypeStruct((layers, rows, n * share), BF16),
                jax.ShapeDtypeStruct((layers, rows, n * share), BF16),
                jax.ShapeDtypeStruct((layers, share, d), BF16),
                jax.ShapeDtypeStruct((8, 128), F32),
            ),
            in_specs=[pl.BlockSpec(memory_space=pl.ANY)] * 2 + [pl.BlockSpec(memory_space=pltpu.VMEM)] * 3,
            out_specs=(pl.BlockSpec(memory_space=pltpu.VMEM),) * 4,
            scratch_shapes=[
                pltpu.VMEM((tokens, d), BF16),
                pltpu.VMEM((tokens, d), BF16),
                pltpu.VMEM((d, tokens), BF16),
                pltpu.VMEM((tokens, d), BF16),
                pltpu.VMEM((d, tokens), BF16),
                pltpu.VMEM((tokens, d), BF16),
                pltpu.VMEM((d, tokens), BF16),
                pltpu.VMEM((tokens, d), F32),
                pltpu.VMEM((chunks, rows + SHARE, d), BF16),
                pltpu.VMEM((chunks, n, rows + SHARE, d), BF16),
                pltpu.VMEM((3, n, rows + SHARE, d), BF16),
                pltpu.VMEM((slots, hops, rows + SHARE, d), BF16),
                pltpu.VMEM((d, 2 * width), F32),
                pltpu.VMEM((d, width), F32),
                pltpu.VMEM((8, d), F32),
                pltpu.VMEM((n, 8, 128), F32),
                dma((chunks, hops)),
                dma((chunks, hops)),
                dma((chunks,)),
                dma((chunks,)),
                dma,
                dma((2, tokens // TILE)),
                dma((slots, hops)),
                dma((slots, hops)),
                dma((n,)),
                dma((n,)),
            ],
            compiler_params=pltpu.CompilerParams(collective_id=0, has_side_effects=True, vmem_limit_bytes=67043328),
            name="step",
        )(x[0], dy[0], *weights)

        def gathered(part):
            part = part.reshape(layers * rows, n * share)
            return lax.dot_general(part, onehot, (((1,), (1,)), ((), ())), preferred_element_type=F32).reshape(layers, rows, -1)

        factor = factor[0, 0]
        gradients = [factor * g for g in (gathered(g_gate), gathered(g_up), g_down.astype(F32))]
        new = [adamw(w.astype(F32), m, v, g) for w, m, v, g in zip(weights, m, v, gradients, strict=True)]
        return tuple(one[which] for which in range(3) for one in new)

    states, cut = P(("rep", "dp"), None, None), P(None, "dp", None)
    return jax.shard_map(
        step,
        mesh=mesh,
        in_specs=(states, states) + (cut,) * 9,
        out_specs=(P("rep", "dp", None),) * 9,
        check_vma=False,
    )
```

time: 275 us -> 221 us (0.80)
  Pallas kernels: 251 us -> 207 us
  local copies, waits for them, and re-layouts: 5.33 us -> 1.45 us
  matrix products: 12.5 us -> 9.64 us
    pallas_call x1, Pallas kernels: 251 us -> 207 us  [step(): pl.pallas_call(functools.partial(kernel, n, steps), out_shape=(jax.ShapeD...]
    dot_general x2 -> x0, matrix products: 4.33 us -> none  [dot(): return jnp.dot(a, b, preferred_element_type=F32)]
where the time goes in v2:
time: 221 us
  Pallas kernels  207 us (94%)
  matrix products  9.64 us (4%)
    pallas_call x1, Pallas kernels, step(): pl.pallas_call(functools.partial(kernel, n, steps), out_shape=(jax.ShapeD...  207 us
    dot_general x2, matrix products, gathered(): lax.dot_general(part, onehot, (((1,), (1,)), ((), ())), preferred_element...  9.64 us

profile of v2, /device:TPU:30, one launch (start us, length us, event | category | flops | bytes accessed | tf_op | source)
XLA Modules:
  0.0 221.1 jit_solution(867202959484580538)
XLA Ops:
  0.6 207.1 %step.1 = (bf16[2,64,1408]{2,1,0:T(8,128)(2,1)}, bf16[2,64,1408]{2,1,0:T(8,128)(2,1)}, bf16[2,176,512]{2,1,0:T(8,128)(2,1)}, f32[8,128]{1,0:T(8,128)}) custom-call(bf16[4096,512]{1,0:T(8,128)(2,1)} %bitcast.17, bf16[4096,512]{1,0:T(8,128)(2,1)} %bitcast.18, bf16[2,64,1408]{2,1,0:T(8,128)(2,1)} %wg_ref.1, bf16[2,64,1408]{2,1,0:T(8,128)(2,1)} %wu_ref.1, ...), custom_call_target="tpu_custom_call" | custom-call | tf_op jit(solution)/shard_map/step/pallas_call | solution.py:429
  207.8 0.0 copy-start.3
  207.8 0.0 copy-start.5
  207.8 0.0 copy-start.6
  207.8 0.0 copy-start.7
  207.8 1.4 slice.3
  209.3 5.5 %fusion.18 = (bf16[2,64,1408]{2,1,0:T(8,128)(2,1)}, f32[2,64,1408]{2,1,0:T(8,128)}, f32[2,64,1408]{2,1,0:T(8,128)}) fusion(bf16[2,64,1408]{2,1,0:T(8,128)(2,1)} %wu_ref.1, f32[2,64,1408]{2,1,0:T(8,128)} %param.20, f32[2,64,1408]{2,1,0:T(8,128)} %param.17, bf16[2,64,1408]{2,1,0:T(8,128)(2,1)} %get-tuple-element.15, s32[1408]{0:T(1024)S(1)} %fusion.33, ...), kind=kOutput, calls=%fused_computation.22 | convolution fusion | flops 512376832 | bytes 3970564 | tf_op jit(solution)/shard_map/dot_general | solution.py:473
  214.8 0.0 copy-start
  214.8 0.0 copy-start.1
  214.8 0.0 copy-start.2
  214.8 0.0 copy-start.4
  214.8 0.0 copy-done.3
  214.8 0.0 copy-done.5
  214.8 0.0 copy-done.6
  214.8 0.0 copy-done.7
  214.9 4.1 %fusion.15 = (bf16[2,64,1408]{2,1,0:T(8,128)(2,1)}, f32[2,64,1408]{2,1,0:T(8,128)}, f32[2,64,1408]{2,1,0:T(8,128)}) fusion(bf16[2,64,1408]{2,1,0:T(8,128)(2,1)S(1)} %copy-done.3, f32[2,64,1408]{2,1,0:T(8,128)S(1)} %copy-done.5, f32[2,64,1408]{2,1,0:T(8,128)S(1)} %copy-done.6, bf16[2,64,1408]{2,1,0:T(8,128)(2,1)S(1)} %copy-done.7, s32[1408]{0:T(1024)S(1)} %fusion.33, ...), kind=kOutput, calls=%fused_computation.19 | convolution fusion | flops 512376832 | bytes 3970564 | tf_op jit(solution)/shard_map/dot_general | solution.py:473
  219.0 0.0 copy-done
  219.0 0.0 copy-done.1
  219.0 0.0 copy-done.2
  219.0 0.0 copy-done.4
  219.0 2.1 fusion.21
  (1 shorter events, 0.0 us)
Async XLA Ops:
  207.8 7.0 %copy-start.3 = (bf16[2,64,1408]{2,1,0:T(8,128)(2,1)S(1)}, bf16[2,64,1408]{2,1,0:T(8,128)(2,1)}, u32[]{:S(2)}) copy-start(bf16[2,64,1408]{2,1,0:T(8,128)(2,1)} %wg_ref.1) | copy-start | bytes 1081348
  207.8 7.0 %copy-start.5 = (f32[2,64,1408]{2,1,0:T(8,128)S(1)}, f32[2,64,1408]{2,1,0:T(8,128)}, u32[]{:S(2)}) copy-start(f32[2,64,1408]{2,1,0:T(8,128)} %param.19) | copy-start | bytes 2162692
  207.8 7.0 %copy-start.6 = (f32[2,64,1408]{2,1,0:T(8,128)S(1)}, f32[2,64,1408]{2,1,0:T(8,128)}, u32[]{:S(2)}) copy-start(f32[2,64,1408]{2,1,0:T(8,128)} %param.16) | copy-start | bytes 2162692
  207.8 7.0 %copy-start.7 = (bf16[2,64,1408]{2,1,0:T(8,128)(2,1)S(1)}, bf16[2,64,1408]{2,1,0:T(8,128)(2,1)}, u32[]{:S(2)}) copy-start(bf16[2,64,1408]{2,1,0:T(8,128)(2,1)} %get-tuple-element.14) | copy-start | bytes 1081348
  214.8 4.2 %copy-start = (bf16[2,176,512]{2,1,0:T(8,128)(2,1)S(1)}, bf16[2,176,512]{2,1,0:T(8,128)(2,1)}, u32[]{:S(2)}) copy-start(bf16[2,176,512]{2,1,0:T(8,128)(2,1)} %wd_ref.1) | copy-start | bytes 1081348
  214.8 4.2 %copy-start.1 = (f32[2,176,512]{2,1,0:T(8,128)S(1)}, f32[2,176,512]{2,1,0:T(8,128)}, u32[]{:S(2)}) copy-start(f32[2,176,512]{2,1,0:T(8,128)} %param.21) | copy-start | bytes 2162692
  214.8 4.2 %copy-start.2 = (f32[2,176,512]{2,1,0:T(8,128)S(1)}, f32[2,176,512]{2,1,0:T(8,128)}, u32[]{:S(2)}) copy-start(f32[2,176,512]{2,1,0:T(8,128)} %param.18) | copy-start | bytes 2162692
  214.8 4.2 %copy-start.4 = (bf16[2,176,512]{2,1,0:T(8,128)(2,1)S(1)}, bf16[2,176,512]{2,1,0:T(8,128)(2,1)}, u32[]{:S(2)}) copy-start(bf16[2,176,512]{2,1,0:T(8,128)(2,1)} %get-tuple-element.16) | copy-start | bytes 1081348

commit v3 on v2

--- a/solution.py
+++ b/solution.py
@@ -260,13 +260,14 @@
         stage(i, 0)
         if 1 <= i <= far:
             pl.loop(tiles * (i - 1) // far, tiles * i // far)(start_tile)
-        stage(i, 1)
+        if i < ahead:
+            stage(i, 1)
 
     acc[...] = jnp.zeros_like(acc)
 
     def forward(s, narrow):
         ready(s, narrow)
-        size = BIG // 2 if narrow else BIG
+        size = BIG
         count, big = cut_by(size)
 
         @pl.loop(0, count)
@@ -276,6 +277,8 @@
             gate, up = gu[:, :units], gu[:, units:]
             act = gate * (0.5 * jnp.tanh(0.5 * gate) + 0.5) * up
             acc[big(t)] += dot(act.astype(BF16), w_d(s, narrow))
+            if not narrow:
+                pl.when(jnp.logical_and(s == 0, t == count // 2 - 1))(lambda: stage(ahead, 1))
             pl.when(t == count // 2 - 1)(lambda: stage(s + ahead + 1, 0))
             pl.when(t == count - 1)(lambda: stage(s + ahead + 1, 1))
 
@@ -302,7 +305,7 @@
             q, u = first + s, base + s
             if whole:
                 ready(u, narrow)
-            count, big = cut_by(BIG // 2 if narrow else BIG)
+            count, big = cut_by(BIG)
             units = width // 2 if narrow else width
 
             @pl.loop(0, count)
@@ -342,6 +345,8 @@
                 dgu[...] = jnp.zeros_like(dgu)
                 ddt[...] = jnp.zeros_like(ddt)
             rs_hop(q, 0, narrow)
+            if narrow and not whole:
+                rs_hop(q - 2, 3, False)
 
         @pl.loop(0, steps - 1)
         def _(s):
@@ -364,7 +369,7 @@
     backward(steps, a0, a0t, False)
 
     for q in range(chunks, chunks + 3):
-        for slot in (1, 2, 3):
+        for slot in (1, 2, 3)[q == chunks :]:
             rs_slot(q, slot)
         rs_end(q)
 
@@ -396,12 +401,41 @@
         sized(u, lambda narrow: sent(narrow, u))
 
 
-def grouped(n, share):
-    steps = -(-share // SHARE)
-    f = jnp.arange(n * share, dtype=jnp.int32)
-    k, s, r = f // share, f % share // SHARE, f % share % SHARE
-    to = s * (n * SHARE) + k * jnp.minimum(SHARE, share - s * SHARE) + r
-    return (to[:, None] == f[None, :]).astype(BF16), steps
+def update(n, f_ref, gg_ref, gu_ref, gd_ref, *refs):
+    given, new, held, (in_sem, out_sem) = refs[:9], refs[9:18], refs[18:27], refs[27:]
+    layers, rows, hidden = gg_ref.shape
+    share = gd_ref.shape[1]
+
+    def fetch(k, l):
+        return pltpu.make_async_copy(given[k].at[l], held[k].at[l], in_sem.at[k, l])
+
+    def put(k, l):
+        return pltpu.make_async_copy(held[k].at[l], new[k].at[l], out_sem.at[k, l])
+
+    for i in range(3):
+        for l in range(layers):
+            for k in (i, 3 + i, 6 + i):
+                fetch(k, l).start()
+    f = lax.broadcasted_iota(jnp.int32, (1, hidden), 1)
+    first = f % share // SHARE * SHARE
+    to = first * n + f // share * jnp.minimum(SHARE, share - first) + f % share - first
+    pick = jnp.where(lax.broadcasted_iota(jnp.int32, (hidden, hidden), 0) == to, 1.0, 0.0).astype(BF16)
+    both = jnp.concatenate([gg_ref[...].reshape(layers * rows, hidden), gu_ref[...].reshape(layers * rows, hidden)], 0)
+    both = dot(both, pick).reshape(2, layers, rows, hidden)
+    factor = f_ref[:1, :1]
+    for i in range(3):
+        for l in range(layers):
+            ks = (i, 3 + i, 6 + i)
+            for k in ks:
+                fetch(k, l).wait()
+            w, m, v = (held[k].at[l] for k in ks)
+            g = factor * (gd_ref[l].astype(F32) if i == 2 else both[i, l])
+            w[...], m[...], v[...] = adamw(w[...].astype(F32), m[...], v[...], g)
+            for k in ks:
+                put(k, l).start()
+    for k in range(9):
+        for l in range(layers):
+            put(k, l).wait()
 
 
 def adamw(w, m, v, g):
@@ -415,12 +449,11 @@
     n = mesh.shape["dp"]
 
     def step(x, dy, *arrays):
-        weights, m, v = (arrays[i : i + 3] for i in (0, 3, 6))
-        w_gate, w_up, w_down = weights
+        w_gate, w_up, w_down = arrays[:3]
         layers, rows, _ = w_gate.shape
         share, d = w_down.shape[1:]
         tokens = x.shape[1]
-        onehot, steps = grouped(n, share)
+        steps = -(-share // SHARE)
         width = n * SHARE
         chunks = layers * steps
 
@@ -466,16 +499,17 @@
             ],
             compiler_params=pltpu.CompilerParams(collective_id=0, has_side_effects=True, vmem_limit_bytes=67043328),
             name="step",
-        )(x[0], dy[0], *weights)
-
-        def gathered(part):
-            part = part.reshape(layers * rows, n * share)
-            return lax.dot_general(part, onehot, (((1,), (1,)), ((), ())), preferred_element_type=F32).reshape(layers, rows, -1)
-
-        factor = factor[0, 0]
-        gradients = [factor * g for g in (gathered(g_gate), gathered(g_up), g_down.astype(F32))]
-        new = [adamw(w.astype(F32), m, v, g) for w, m, v, g in zip(weights, m, v, gradients, strict=True)]
-        return tuple(one[which] for which in range(3) for one in new)
+        )(x[0], dy[0], w_gate, w_up, w_down)
+
+        held = [pltpu.VMEM(one.shape, one.dtype) for one in arrays]
+        return pl.pallas_call(
+            functools.partial(update, n),
+            out_shape=tuple(jax.ShapeDtypeStruct(one.shape, one.dtype) for one in arrays),
+            in_specs=[pl.BlockSpec(memory_space=pltpu.VMEM)] * 4 + [pl.BlockSpec(memory_space=pl.ANY)] * 9,
+            out_specs=(pl.BlockSpec(memory_space=pl.ANY),) * 9,
+            scratch_shapes=held + [dma((9, layers)), dma((9, layers))],
+            name="update",
+        )(factor, g_gate, g_up, g_down, *arrays)
 
     states, cut = P(("rep", "dp"), None, None), P(None, "dp", None)
     return jax.shard_map(

time: 221 us -> 212 us (0.959)
  matrix products: 9.64 us -> 0 us
  Pallas kernels: 207 us -> 211 us
    dot_general x2 -> x0, matrix products: 9.64 us -> none  [gathered(): lax.dot_general(part, onehot, (((1,), (1,)), ((), ())), preferred_element...]
    pallas_call x0 -> x1, Pallas kernels: none -> 5.67 us  [step(): pl.pallas_call(functools.partial(update, n), out_shape=tuple((jax.ShapeDt...]
where the time goes in v3:
time: 212 us
  Pallas kernels  211 us (100%)
    pallas_call x1, Pallas kernels, step(): pl.pallas_call(functools.partial(kernel, n, steps), out_shape=(jax.ShapeD...  205 us
    pallas_call x1, Pallas kernels, step(): pl.pallas_call(functools.partial(update, n), out_shape=tuple((jax.ShapeDt...  5.67 us

profile of v3, /device:TPU:30, one launch (start us, length us, event | category | flops | bytes accessed | tf_op | source)
XLA Modules:
  0.0 212.0 jit_solution(2143241963393125375)
XLA Ops:
  0.6 205.5 %step.1 = (bf16[2,64,1408]{2,1,0:T(8,128)(2,1)}, bf16[2,64,1408]{2,1,0:T(8,128)(2,1)}, bf16[2,176,512]{2,1,0:T(8,128)(2,1)}, f32[8,128]{1,0:T(8,128)}) custom-call(bf16[4096,512]{1,0:T(8,128)(2,1)} %bitcast.2, bf16[4096,512]{1,0:T(8,128)(2,1)} %bitcast.3, bf16[2,64,1408]{2,1,0:T(8,128)(2,1)} %refs_0_.1, bf16[2,64,1408]{2,1,0:T(8,128)(2,1)} %refs_1_.1, ...), custom_call_target="tpu_custom_call" | custom-call | tf_op jit(solution)/shard_map/step/pallas_call | solution.py:462
  206.1 5.7 %update.1 = (bf16[2,64,1408]{2,1,0:T(8,128)(2,1)}, bf16[2,64,1408]{2,1,0:T(8,128)(2,1)}, bf16[2,176,512]{2,1,0:T(8,128)(2,1)}, f32[2,64,1408]{2,1,0:T(8,128)}, f...) custom-call(f32[8,128]{1,0:T(8,128)} %get-tuple-element.13.f_ref, ...), custom_call_target="tpu_custom_call" | custom-call | tf_op jit(solution)/shard_map/update/pallas_call | solution.py:505
